TPU v7x, 32 devices: a whole 2x2x4 slice. The times are simulated.
32 devices in a mesh: dp: 2 (over x), fsdp: 16 (over z, y, core).
Axes of the slice: x: 2, y: 2, z: 4, core: 2. Of those that a mesh axis runs over, the one named last changes fastest.
Arguments:
- inputs: bfloat16 [32, 512, 768], P(('dp', 'fsdp')), may hold values from -6 to 6
- segments: int32 [32, 512], P(('dp', 'fsdp')), may hold values from 0 to 3, never falling along the last dimension, each value on 1 to 256 neighbouring positions
- out_grads: bfloat16 [4, 32, 512, 768], P(None, ('dp', 'fsdp')), may hold values from -6 to 6
- query_weight: bfloat16 [768, 768], P(('dp', 'fsdp')), may hold values from -0.21875 to 0.21875
- query_bias: bfloat16 [768], P(('dp', 'fsdp')), may hold values from -1.1953125 to 1.1953125
- key_weight: bfloat16 [768, 768], P(('dp', 'fsdp')), may hold values from -0.21875 to 0.21875
- value_weight: bfloat16 [768, 768], P(('dp', 'fsdp')), may hold values from -0.21875 to 0.21875
- value_bias: bfloat16 [768], P(('dp', 'fsdp')), may hold values from -1.1953125 to 1.1953125
- output_weight: bfloat16 [768, 768], P(('dp', 'fsdp')), may hold values from -2.5 to 2.5
- output_bias: bfloat16 [768], P(('dp', 'fsdp')), may hold values from -1.1953125 to 1.1953125
- first_gain: bfloat16 [768], P(('dp', 'fsdp')), may hold values from 0.5 to 1.5
- first_shift: bfloat16 [768], P(('dp', 'fsdp')), may hold values from -1.1953125 to 1.1953125
- inner_weight: bfloat16 [768, 3072], P(('dp', 'fsdp')), may hold values from -0.21875 to 0.21875
- inner_bias: bfloat16 [3072], P(('dp', 'fsdp')), may hold values from -1.1953125 to 1.1953125
- outer_weight: bfloat16 [3072, 768], P(('dp', 'fsdp')), may hold values from -0.21875 to 0.21875
- outer_bias: bfloat16 [768], P(('dp', 'fsdp')), may hold values from -1.1953125 to 1.1953125
- second_gain: bfloat16 [768], P(('dp', 'fsdp')), may hold values from 0.5 to 1.5
- second_shift: bfloat16 [768], P(('dp', 'fsdp')), may hold values from -1.1953125 to 1.1953125
Outputs:
- outputs: bfloat16 [4, 32, 512, 768], P(None, ('dp', 'fsdp'))
- input_grad: float32 [32, 512, 768], P(('dp', 'fsdp'))
- query_weight_grad: float32 [768, 768], P(('dp', 'fsdp'))
- query_bias_grad: float32 [768], P(('dp', 'fsdp'))
- key_weight_grad: float32 [768, 768], P(('dp', 'fsdp'))
- value_weight_grad: float32 [768, 768], P(('dp', 'fsdp'))
- value_bias_grad: float32 [768], P(('dp', 'fsdp'))
- output_weight_grad: float32 [768, 768], P(('dp', 'fsdp'))
- output_bias_grad: float32 [768], P(('dp', 'fsdp'))
- first_gain_grad: float32 [768], P(('dp', 'fsdp'))
- first_shift_grad: float32 [768], P(('dp', 'fsdp'))
- inner_weight_grad: float32 [768, 3072], P(('dp', 'fsdp'))
- inner_bias_grad: float32 [3072], P(('dp', 'fsdp'))
- outer_weight_grad: float32 [3072, 768], P(('dp', 'fsdp'))
- outer_bias_grad: float32 [768], P(('dp', 'fsdp'))
- second_gain_grad: float32 [768], P(('dp', 'fsdp'))
- second_shift_grad: float32 [768], P(('dp', 'fsdp'))
Inputs may be any that keep to these rules, and one draw needn't show every extreme that they name: `segments`: in each row the segment numbers start at 0, never fall, and each of the 4 examples holds 1 to 256 tokens.
All inputs are finite; a program needn't handle non-finite values.
Results may differ from a plain program's by a relative error of at most 0.014.
Values may be sent and summed in bfloat16 or wider, within the bound.
A program may use at most 256 MiB of HBM per device.

v0:
```python
import functools

import jax
import jax.numpy as jnp
from jax import lax
from jax.experimental import pallas as pl
from jax.experimental.pallas import tpu as pltpu
from jax.sharding import PartitionSpec as P

HEADS = 12
DH = 64
WIDTHS = 4
EPSILON = 1e-12
SCORE_SCALE = 0.125
MASKED = -1000000000.0
BF = jnp.bfloat16
F32 = jnp.float32
AXES = ("dp", "fsdp")
EXTRA = 128


def dot(a, b):
    return jnp.dot(a, b, preferred_element_type=F32)


def dot_tn(a, b):
    return lax.dot_general(a, b, (((0,), (0,)), ((), ())), preferred_element_type=F32)


def dot_nt(a, b):
    return lax.dot_general(a, b, (((1,), (1,)), ((), ())), preferred_element_type=F32)


MESH = pl.DeviceIdType.MESH
HALF = 384
SMALL = 2304
OUT = SMALL + EXTRA


class Place:
    def __init__(self):
        self.x = lax.axis_index("dp")
        f = lax.axis_index("fsdp")
        self.z = f // 4
        self.y = (f // 2) % 2
        self.c = f % 2

    def ident(self, x=None, z=None, y=None, c=None):
        x = self.x if x is None else x
        z = self.z if z is None else z
        y = self.y if y is None else y
        c = self.c if c is None else c
        return {"dp": x, "fsdp": z * 4 + y * 2 + c}

    def index(self, x=None, z=None, y=None, c=None):
        x = self.x if x is None else x
        z = self.z if z is None else z
        y = self.y if y is None else y
        c = self.c if c is None else c
        return x * 16 + z * 4 + y * 2 + c


def greet(place):
    barrier = pltpu.get_barrier_semaphore()
    others = [place.ident(z=lax.rem(place.z + o, 4)) for o in (1, 2, 3)]
    others += [place.ident(x=1 - place.x), place.ident(y=1 - place.y), place.ident(c=1 - place.c)]
    for other in others:
        pl.semaphore_signal(barrier, inc=1, device_id=other, device_id_type=MESH)
    pl.semaphore_wait(barrier, len(others))


def chunk_list(parts, order_first):
    return parts


def gather_kernel(chunks, ins, outs, send_sem, recv_sem, own_sem):
    place = Place()
    greet(place)
    me = place.index()
    counts = [0] * len(chunks)

    def mine(ci):
        a, rows, r0, nr, c0, nc, order = chunks[ci]
        return ins[a].at[pl.ds(r0, nr), pl.ds(c0, nc)]

    def slot(ci, shard):
        a, rows, r0, nr, c0, nc, order = chunks[ci]
        return outs[a].at[pl.ds(pl.multiple_of(shard * rows + r0, 8), nr), pl.ds(c0, nc)]

    pending = []

    def send(ci, shard, to, first=False):
        n = counts[ci]
        counts[ci] += 1
        cp = pltpu.make_async_remote_copy(
            src_ref=mine(ci) if first else slot(ci, shard),
            dst_ref=slot(ci, shard),
            send_sem=send_sem.at[ci, n],
            recv_sem=recv_sem.at[ci, shard],
            device_id=to,
            device_id_type=MESH,
        )
        cp.start()
        pending.append(cp)

    def arrived(ci, shard):
        pltpu.make_async_remote_copy(
            src_ref=slot(ci, shard),
            dst_ref=slot(ci, shard),
            send_sem=send_sem.at[ci, 0],
            recv_sem=recv_sem.at[ci, shard],
            device_id=place.ident(c=1 - place.c),
            device_id_type=MESH,
        ).wait_recv()

    def near(order):
        nx, ny = {"x": 1 - place.x}, {"y": 1 - place.y}
        return (ny, nx) if order == 0 else (nx, ny)

    sib = place.ident(c=1 - place.c)
    zs = [lax.rem(place.z + o, 4) for o in (1, 2, 3)]
    for ci in range(len(chunks)):
        n1, n2 = near(chunks[ci][-1])
        for z in zs:
            send(ci, me, place.ident(z=z), True)
        send(ci, me, place.ident(**n1), True)
        send(ci, me, place.ident(**n2), True)
        send(ci, me, sib, True)
    for ci in range(len(chunks)):
        cp = pltpu.make_async_copy(mine(ci), slot(ci, me), own_sem.at[ci])
        cp.start()

    def from_n1(ci, z):
        n1, n2 = near(chunks[ci][-1])
        shard = place.index(z=z, **n1)
        arrived(ci, shard)
        send(ci, shard, place.ident(**n2))
        send(ci, shard, sib)

    def step2(ci):
        n1, n2 = near(chunks[ci][-1])
        from_n1(ci, place.z)
        for z in zs:
            shard = place.index(z=z)
            arrived(ci, shard)
            send(ci, shard, place.ident(**n1))
            send(ci, shard, place.ident(**n2))
            send(ci, shard, sib)

    def step3(ci):
        for z in zs:
            from_n1(ci, z)

    def step4(ci):
        n1, n2 = near(chunks[ci][-1])
        for far in ({}, n1):
            for z in [place.z] + zs:
                shard = place.index(z=z, **n2, **far)
                arrived(ci, shard)
                send(ci, shard, sib)

    pairs = [list(range(i, min(i + 2, len(chunks)))) for i in range(0, len(chunks), 2)]
    for t in range(len(pairs) + 2):
        for stage, fn in ((0, step2), (1, step3), (2, step4)):
            if 0 <= t - stage < len(pairs):
                for ci in pairs[t - stage]:
                    fn(ci)
    for ci in range(len(chunks)):
        for x in range(2):
            for y in range(2):
                for z in range(4):
                    arrived(ci, place.index(x=x, y=y, z=z, c=1 - place.c))
    for ci in range(len(chunks)):
        pltpu.make_async_copy(mine(ci), slot(ci, me), own_sem.at[ci]).wait()
    for cp in pending:
        cp.wait_send()


def gather(arrays, chunks, cid):
    n = len(arrays)

    def kernel(*refs):
        gather_kernel(chunks, refs[:n], refs[n : 2 * n], *refs[2 * n :])

    return pl.pallas_call(
        kernel,
        out_shape=[jax.ShapeDtypeStruct((32 * a.shape[0], a.shape[1]), a.dtype) for a in arrays],
        in_specs=[pl.BlockSpec(memory_space=pl.ANY)] * n,
        out_specs=[pl.BlockSpec(memory_space=pl.ANY)] * n,
        scratch_shapes=[
            pltpu.SemaphoreType.DMA((len(chunks), 31)),
            pltpu.SemaphoreType.DMA((len(chunks), 32)),
            pltpu.SemaphoreType.DMA((len(chunks),)),
        ],
        compiler_params=pltpu.CompilerParams(collective_id=cid, has_side_effects=True),
        name="gather",
    )(*arrays)


SLOT0 = (0, 4, 7, 9)
LN_ROWS = 64


def lanes(shape):
    return lax.broadcasted_iota(jnp.int32, shape, 1)


def row_loop(seq, body):
    @pl.loop(0, seq // LN_ROWS)
    def _(t):
        body(pl.ds(pl.multiple_of(t * LN_ROWS, LN_ROWS), LN_ROWS))


def spread_mats(dim):
    r = lax.broadcasted_iota(jnp.int32, (dim // 4, dim), 0)
    h = lax.broadcasted_iota(jnp.int32, (dim // 4, dim), 1)
    return [jnp.where(h == 4 * r + c, 1.0, 0.0).astype(BF) for c in range(4)]


def fwd_steps(r):
    seq, dim = r.x.shape
    hid = r.wi.shape[1] // WIDTHS
    vec = r.vec

    def small():
        sm = r.wp[:, SMALL:OUT].astype(F32).T
        vec[0:16, :] = sm[0:16]
        mats = spread_mats(dim)
        part = dim // WIDTHS
        for j in range(WIDTHS):
            row = jnp.zeros((8, dim), F32)
            for c in range(4):
                lhs = jnp.broadcast_to(sm[8 + c : 9 + c, part * j : part * (j + 1)], (8, part)).astype(BF)
                row = row + dot(lhs, mats[c])
            vec[16 + j : 17 + j, :] = row[0:1]

    def qkv():
        for t, bias in ((0, 0), (1, None), (2, 1)):
            for h in range(2):
                at = 3 * HALF * h + HALF * t
                acc = dot(r.x[...], r.wp[:, at : at + HALF])
                if bias is not None:
                    acc = acc + vec[bias : bias + 1, HALF * h : HALF * (h + 1)]
                r.qkv[t, :, HALF * h : HALF * (h + 1)] = acc.astype(BF)

    def attention():
        same = r.segc[...] == r.segr[...]

        @pl.loop(0, HEADS // 2)
        def _(i):
            cols = pl.ds(pl.multiple_of(i * 128, 128), 128)
            q, k, v = r.qkv[0, :, cols], r.qkv[1, :, cols], r.qkv[2, :, cols]
            low = lanes(q.shape) < DH
            zero = jnp.zeros_like(q)
            outs = []
            lse = r.lse[...]
            for half in range(2):
                qh = jnp.where(low if half == 0 else ~low, q, zero)
                s = jnp.where(same, dot_nt(qh, k) * SCORE_SCALE, MASKED)
                m = jnp.max(s, axis=-1, keepdims=True)
                e = jnp.exp(s - m)
                total = jnp.sum(e, axis=-1, keepdims=True)
                p = (e * (1.0 / total)).astype(BF)
                outs.append(dot(p, v))
                lse = jnp.where(lanes(lse.shape) == 2 * i + half, m + jnp.log(total), lse)
            r.lse[...] = lse
            r.att[:, cols] = jnp.where(low, outs[0], outs[1]).astype(BF)

    def norm1():
        feat = dim // WIDTHS
        for k in range(WIDTHS):
            lo = (feat * k // 128) * 128
            win = r.att[:, lo : lo + 256]
            at = lanes(win.shape) + lo
            win = jnp.where((at >= feat * k) & (at < feat * (k + 1)), win, jnp.zeros_like(win))
            add = dot(win, r.wp[lo : lo + 256, OUT : OUT + dim])
            r.br[...] = add if k == 0 else r.br[...] + add

            def body(rows, k=k):
                h = r.x[rows, :].astype(F32) + r.br[rows, :] + vec[2:3, :]
                c = h - jnp.mean(h, axis=-1, keepdims=True)
                inv = lax.rsqrt(jnp.mean(c * c, axis=-1, keepdims=True) + EPSILON)
                sc = c * inv
                first = sc * vec[3:4, :] + vec[4:5, :]
                r.first[k, rows, :] = first
                r.low[k, rows, :] = first.astype(BF)
                r.sc[k, rows, :] = sc.astype(BF)
                r.inv[rows, k : k + 1] = inv

            row_loop(seq, body)

    def inner():
        @pl.loop(0, WIDTHS)
        def _(j):
            start = lax.div(j * (9 - j), 2)

            @pl.loop(0, hid // 256)
            def _(n):
                cols = pl.ds(pl.multiple_of(n * 256, 256), 256)
                wcols = pl.ds(pl.multiple_of(j * hid + n * 256, 256), 256)
                bias = vec[pl.ds(16 + j, 1), cols]

                @pl.loop(j, WIDTHS)
                def _(k):
                    pre = dot(r.low[k], r.wi[:, wcols]) + bias
                    phi = 0.5 * (1.0 + lax.erf(pre * 0.7071067811865476))
                    slope = phi + pre * (jnp.exp(-0.5 * pre * pre) * 0.3989422804014327)
                    r.act[start + k - j, :, cols] = (pre * phi).astype(BF)
                    r.slope[start + k - j, :, cols] = slope.astype(BF)

    def outer(k):
        def run():
            @pl.loop(0, dim // 256)
            def _(n):
                cols = pl.ds(pl.multiple_of(n * 256, 256), 256)
                acc = dot(r.act[SLOT0[0] + k], r.wu[0:hid, cols])
                for j in range(1, k + 1):
                    acc = acc + dot(r.act[SLOT0[j] + k - j], r.wu[hid * j : hid * (j + 1), cols])
                r.br[:, cols] = acc

            def body(rows):
                h = r.first[k, rows, :] + r.br[rows, :] + vec[5:6, :]
                c = h - jnp.mean(h, axis=-1, keepdims=True)
                inv = lax.rsqrt(jnp.mean(c * c, axis=-1, keepdims=True) + EPSILON)
                sc = c * inv
                r.out[k, rows, :] = (sc * vec[6:7, :] + vec[7:8, :]).astype(BF)
                up = r.up[k, rows, :].astype(F32)
                tg = up * vec[6:7, :]
                ts = tg * sc
                back = inv * (tg - jnp.mean(tg, axis=-1, keepdims=True) - sc * jnp.mean(ts, axis=-1, keepdims=True))
                ob = back.astype(BF)
                r.ob[k, rows, :] = ob
                r.acc[0:1, :] += jnp.sum(up * sc, axis=0, keepdims=True)
                r.acc[1:2, :] += jnp.sum(up, axis=0, keepdims=True)
                r.acc[2:3, :] += jnp.sum(ob.astype(F32), axis=0, keepdims=True)

            row_loop(seq, body)
        return run

    def clear():
        r.acc[...] = jnp.zeros_like(r.acc)
        r.lse[...] = jnp.zeros_like(r.lse)
        r.inv[...] = jnp.zeros_like(r.inv)

    return dict(clear=clear, small=small, qkv=qkv, attention=attention, norm1=norm1, inner=inner,
                outer=[outer(k) for k in range(WIDTHS)])


class Refs:
    pass


def named(names, refs):
    r = Refs()
    for name, ref in zip(names, refs):
        setattr(r, name, ref)
    return r


FWD_IN = ("x", "segc", "segr", "up", "hp", "hi", "hu")
FWD_OUT = ("hout", "hact", "hslope", "hlow", "hob", "hsc", "hqkv", "hatt", "inv", "lse", "vec", "acc")
FWD_SCRATCH = ("wp", "wi", "wu", "qkv", "att", "br", "first", "low", "act", "slope", "out", "ob", "sc", "sem")


def forward(x, segc, segr, up, hp, hi, hu):
    seq, dim = x.shape
    ff = hi.shape[1]
    hid = ff // WIDTHS
    row = (seq, dim)
    names = FWD_IN + FWD_OUT + FWD_SCRATCH

    def kernel(*refs):
        r = named(names, refs)
        s = fwd_steps(r)
        loads = [pltpu.make_async_copy(a, b, r.sem.at[i]) for i, (a, b) in
                 enumerate(((r.hp, r.wp), (r.hi, r.wi), (r.hu, r.wu)))]
        for cp in loads:
            cp.start()
        s["clear"]()
        loads[0].wait()
        s["small"]()
        s["qkv"]()
        s["attention"]()
        s["norm1"]()
        loads[1].wait()
        s["inner"]()
        stores = [pltpu.make_async_copy(a, b, r.sem.at[3 + i]) for i, (a, b) in enumerate(
            ((r.act, r.hact), (r.slope, r.hslope), (r.low, r.hlow), (r.sc, r.hsc), (r.qkv, r.hqkv), (r.att, r.hatt)))]
        for cp in stores:
            cp.start()
        loads[2].wait()
        for k in range(WIDTHS):
            s["outer"][k]()
        late = [pltpu.make_async_copy(r.out, r.hout, r.sem.at[9]), pltpu.make_async_copy(r.ob, r.hob, r.sem.at[10])]
        for cp in late:
            cp.start()
        for cp in stores + late:
            cp.wait()

    any_ = pl.BlockSpec(memory_space=pl.ANY)
    vm = pl.BlockSpec(memory_space=pltpu.VMEM)
    S = jax.ShapeDtypeStruct
    out_shape = [S((4,) + row, BF), S((10, seq, hid), BF), S((10, seq, hid), BF), S((4,) + row, BF), S((4,) + row, BF),
                 S((4,) + row, BF), S((3,) + row, BF), S(row, BF), S((seq, 128), F32), S((seq, 128), F32),
                 S((24, dim), F32), S((24, dim), F32)]
    V = pltpu.VMEM
    return pl.pallas_call(
        kernel,
        out_shape=out_shape,
        in_specs=[vm, vm, vm, vm, any_, any_, any_],
        out_specs=[any_] * 8 + [vm] * 4,
        scratch_shapes=[V(hp.shape, BF), V(hi.shape, BF), V(hu.shape, BF), V((3,) + row, BF), V(row, BF), V(row, F32),
                        V((4,) + row, F32), V((4,) + row, BF), V((10, seq, hid), BF), V((10, seq, hid), BF),
                        V((4,) + row, BF), V((4,) + row, BF), V((4,) + row, BF), pltpu.SemaphoreType.DMA((11,))],
        compiler_params=pltpu.CompilerParams(vmem_limit_bytes=64 * 1000 * 1000),
        name="forward",
    )(x, segc, segr, up, hp, hi, hu)


class Scatter:
    def __init__(self, chunks, src, bufs, sems):
        self.chunks = chunks
        self.src = src
        n = len(chunks)
        self.own, self.rc, self.r1, self.r2, self.rz = (bufs[i * n : (i + 1) * n] for i in range(5))
        self.sems = sems
        self.place = Place()

    def flips(self, ci, i):
        f1, f2, dz = 1 - i // 8, 1 - (i // 4) % 2, lax.rem(i + 1, 4)
        p = self.place
        fx, fy = (f1, f2) if self.chunks[ci][-1] == 0 else (f2, f1)
        return dict(x=lax.rem(p.x + fx, 2), y=lax.rem(p.y + fy, 2), z=lax.rem(p.z + dz, 4))

    def near(self, ci):
        nx, ny = {"x": 1 - self.place.x}, {"y": 1 - self.place.y}
        return (nx, ny) if self.chunks[ci][-1] == 0 else (ny, nx)

    def rows(self, ci, shard):
        a, rows, r0, nr, c0, nc, order = self.chunks[ci]
        return self.src[a].at[pl.ds(pl.multiple_of(shard * rows + r0, 8), nr), pl.ds(c0, nc)]

    def remote(self, ci, src, dst, send, recv, i, to):
        return pltpu.make_async_remote_copy(
            src_ref=src, dst_ref=dst, send_sem=self.sems[send].at[ci, i], recv_sem=self.sems[recv].at[ci, i],
            device_id=to, device_id_type=MESH,
        )

    def core(self, ci, i):
        p = self.place
        shard = p.index(c=1 - p.c, **self.flips(ci, i))
        return self.remote(ci, self.rows(ci, shard), self.rc[ci].at[i], 1, 2, i, p.ident(c=1 - p.c))

    def load(self, ci, i):
        shard = self.place.index(**self.flips(ci, i))
        return pltpu.make_async_copy(self.rows(ci, shard), self.own[ci].at[i], self.sems[0].at[ci, i])

    def first(self, ci, i):
        to = self.place.ident(**self.near(ci)[0])
        return self.remote(ci, self.own[ci].at[i], self.r1[ci].at[i], 3, 4, i, to)

    def second(self, ci, i):
        to = self.place.ident(**self.near(ci)[1])
        return self.remote(ci, self.own[ci].at[8 + i], self.r2[ci].at[i], 5, 6, i, to)

    def along(self, ci, i):
        to = self.place.ident(z=lax.rem(self.place.z + i + 1, 4))
        return self.remote(ci, self.own[ci].at[12 + i], self.rz[ci].at[i], 7, 8, i, to)

    def add(self, ci, i, buf, j):
        self.own[ci][i] = (self.own[ci][i].astype(F32) + buf[ci][j].astype(F32)).astype(BF)

    def start(self, ci):
        @pl.loop(0, 16)
        def _(i):
            self.core(ci, i).start()
            self.load(ci, i).start()

    def stage1(self, ci):
        @pl.loop(0, 16)
        def _(i):
            self.load(ci, i).wait()
            self.core(ci, i).wait_recv()
            self.add(ci, i, self.rc, i)

            @pl.when(i < 8)
            def _():
                self.first(ci, i).start()

    def stage2(self, ci):
        @pl.loop(0, 8)
        def _(i):
            self.first(ci, i).wait_recv()
            self.add(ci, 8 + i, self.r1, i)

            @pl.when(i < 4)
            def _():
                self.second(ci, i).start()

    def stage3(self, ci):
        @pl.loop(0, 4)
        def _(i):
            self.second(ci, i).wait_recv()
            self.add(ci, 12 + i, self.r2, i)

            @pl.when(i < 3)
            def _():
                self.along(ci, i).start()

    def stage4(self, ci):
        total = self.own[ci][15].astype(F32)
        for i in range(3):
            self.along(ci, i).wait_recv()
            total = total + self.rz[ci][i].astype(F32)
        return total

    def finish(self, ci):
        for count, fn in ((16, self.core), (8, self.first), (4, self.second), (3, self.along)):
            @pl.loop(0, count)
            def _(i):
                fn(ci, i).wait_send()


def scatter_chunks(rows, dim, ff):
    u = [(2, 4 * rows, h * 2 * rows, 2 * rows, 0, dim, h) for h in range(2)]
    i = [(1, rows, 0, rows, h * ff // 2, ff // 2, h) for h in range(2)]
    o = [(0, rows, 0, rows, OUT + HALF * h, HALF, h) for h in range(2)]
    q0 = [(0, rows, 0, rows, 0, 640, 0), (0, rows, 0, rows, 640, 512, 1)]
    q1 = [(0, rows, 0, rows, 1152, 640, 0), (0, rows, 0, rows, 1792, 640, 1)]
    return u + i + o + q0 + q1


BWD_IN = ("x", "segc", "segr", "inv", "lse", "vec", "acc0", "hob", "hact", "hslope", "hlow", "hsc", "hu", "hi", "hp",
          "hqkv", "hatt")
BWD_OUT = ("xg", "gp", "gi", "gu")
BWD_SCRATCH = ("ob", "act", "slope", "low", "w", "tot", "acc", "abi", "stage", "sem", "gsem")


def bwd_steps(r, emit):
    seq, dim = r.x.shape
    hid = r.slope.shape[1]
    vec = r.vec
    feat = dim // WIDTHS
    half = dim // 2

    def d_outer(j):
        for m in range(hid // half):
            lhs = r.act[SLOT0[j] * seq : (SLOT0[j] + WIDTHS - j) * seq, m * half : (m + 1) * half]
            emit(2, dot_tn(lhs, r.ob[j * seq :, :]), hid * j + m * half, 0)

    def inner_back(first, last):
        @pl.loop(first, last)
        def _(j):
            start = lax.div(j * (9 - j), 2)

            @pl.loop(0, hid // 256)
            def _(n):
                cols = pl.ds(pl.multiple_of(n * 256, 256), 256)
                wrows = pl.ds(pl.multiple_of(j * hid + n * 256, 256), 256)

                @pl.loop(j, WIDTHS)
                def _(k):
                    rows = pl.ds(pl.multiple_of((start + k - j) * seq, seq), seq)
                    grad = dot_nt(r.ob[pl.ds(pl.multiple_of(k * seq, seq), seq), :], r.w[wrows, :])
                    ib = (grad * r.slope[rows, cols].astype(F32)).astype(BF)
                    r.slope[rows, cols] = ib
                    r.abi[pl.ds(j, 1), cols] += jnp.sum(ib.astype(F32), axis=0, keepdims=True)

    def d_inner(j):
        for m in range(dim // half):
            lhs = r.low[j * seq :, m * half : (m + 1) * half]
            emit(1, dot_tn(lhs, r.slope[SLOT0[j] * seq : (SLOT0[j] + WIDTHS - j) * seq, :]), m * half, hid * j)

    def first_back(k):
        def slot(j):
            at = (SLOT0[j] + k - j) * seq
            return r.slope[at : at + seq, :]

        @pl.loop(0, dim // 256)
        def _(n):
            cols = pl.ds(pl.multiple_of(n * 256, 256), 256)
            acc = r.ob[k * seq : (k + 1) * seq, cols].astype(F32)
            for j in range(k + 1):
                acc = acc + dot_nt(slot(j), r.w[pl.ds(pl.multiple_of(n * 256 + dim * j, 256), 256), :])
            r.xg[:, cols] = acc

        def body(rows):
            fb = r.xg[rows, :]
            at = pl.ds(rows.start + k * seq, LN_ROWS)
            sc = r.act[at, :].astype(F32)
            fs = fb * sc
            r.acc[3:4, :] += jnp.sum(fs, axis=0, keepdims=True)
            r.acc[4:5, :] += jnp.sum(fb, axis=0, keepdims=True)
            gain = vec[3:4, :]
            tg = fb * gain
            ab = r.inv[rows, k : k + 1] * (
                tg - jnp.mean(tg, axis=-1, keepdims=True) - sc * jnp.mean(fs * gain, axis=-1, keepdims=True))
            tot = ab if k == WIDTHS - 1 else r.tot[rows, :] + ab
            r.tot[rows, :] = tot
            r.act[pl.ds(rows.start + k * seq, LN_ROWS), :] = tot.astype(BF)
            if k == 0:
                r.acc[5:6, :] += jnp.sum(tot, axis=0, keepdims=True)

        row_loop(seq, body)

    def suffix(k):
        return r.act[k * seq : (k + 1) * seq, :]

    def d_output():
        for m in range(2):
            lhs = r.low[3 * seq :, m * half : (m + 1) * half]
            one = dot_tn(lhs, suffix(2 * m))
            two = dot_tn(lhs, suffix(2 * m + 1))
            emit(0, jnp.concatenate([one[:feat], two[feat:]], axis=0), m * half, OUT)

    def att_back():
        for m in range(2):
            w = r.w[3 * dim + m * half : 3 * dim + (m + 1) * half, :]
            one = dot_nt(suffix(2 * m), w)
            two = dot_nt(suffix(2 * m + 1), w)
            r.act[4 * seq : 5 * seq, m * half : (m + 1) * half] = jnp.where(
                lanes(one.shape) < feat, one, two).astype(BF)

    def attention_back(first, last):
        same = r.segc[...] == r.segr[...]

        @pl.loop(first, last)
        def _(i):
            cols = pl.ds(pl.multiple_of(i * 128, 128), 128)
            q, k, v = r.low[0:seq, cols], r.low[seq : 2 * seq, cols], r.low[2 * seq : 3 * seq, cols]
            g = r.act[4 * seq : 5 * seq, cols]
            low = lanes(q.shape) < DH
            zero = jnp.zeros_like(q)
            lse = r.lse[...]
            res = []
            for hf in range(2):
                mine = low if hf == 0 else ~low
                qh = jnp.where(mine, q, zero)
                gh = jnp.where(mine, g, zero)
                s = jnp.where(same, dot_nt(qh, k) * SCORE_SCALE, MASKED)
                col = jnp.sum(jnp.where(lanes(lse.shape) == 2 * i + hf, lse, 0.0), axis=-1, keepdims=True)
                p = jnp.exp(s - col)
                dp = dot_nt(gh, v)
                ds = (p * (dp - jnp.sum(p * dp, axis=-1, keepdims=True))).astype(BF)
                res.append((dot(ds, k), dot_tn(ds, q), dot_tn(p.astype(BF), g)))
            for t, scale in ((0, SCORE_SCALE), (1, SCORE_SCALE), (2, 1.0)):
                r.act[(5 + t) * seq : (6 + t) * seq, cols] = (
                    jnp.where(low, res[0][t], res[1][t]) * scale).astype(BF)

    def d_qkv(h):
        for t in range(3):
            cols = slice(HALF * h, HALF * (h + 1))
            grad = r.act[(5 + t) * seq : (6 + t) * seq, cols]
            for m in range(2):
                emit(0, dot_tn(r.x[:, m * half : (m + 1) * half], grad), m * half, 3 * HALF * h + HALF * t)
            if t != 1:
                r.acc[6 + t // 2 : 7 + t // 2, cols] = jnp.sum(grad.astype(F32), axis=0, keepdims=True)

    def input_grad():
        @pl.loop(0, dim // 256)
        def _(n):
            cols = pl.ds(pl.multiple_of(n * 256, 256), 256)
            acc = r.tot[:, cols]
            for t in range(3):
                acc = acc + dot_nt(r.act[(5 + t) * seq : (6 + t) * seq, :],
                                   r.w[pl.ds(pl.multiple_of(n * 256 + dim * t, 256), 256), :])
            r.xg[:, cols] = acc

    def small():
        mats = spread_mats(dim)
        part = dim // WIDTHS
        bi = r.abi[...].astype(BF)
        rows = []
        for c in range(4):
            moved = [dot_nt(bi, mats[c])[j : j + 1] for j in range(WIDTHS)]
            rows.append(jnp.concatenate(moved, axis=1))
        a = r.acc
        vecs = [a[6:7, :], a[7:8, :], a[5:6, :], a[3:4, :], a[4:5, :], a[2:3, :], a[0:1, :], a[1:2, :]]
        tall = jnp.concatenate(vecs + rows + [jnp.zeros((128 - 12, dim), F32)], axis=0)
        flipped = tall.T
        for m in range(2):
            emit(0, flipped[m * half : (m + 1) * half], m * half, SMALL)

    def clear():
        r.acc[0:3, :] = r.acc0[0:3, :]
        r.acc[3:24, :] = jnp.zeros((21, dim), F32)
        r.abi[...] = jnp.zeros_like(r.abi)

    return dict(clear=clear, d_outer=d_outer, inner_back=inner_back, d_inner=d_inner, first_back=first_back,
                d_output=d_output, att_back=att_back, attention_back=attention_back, d_qkv=d_qkv,
                input_grad=input_grad, small=small)


def backward(x, segc, segr, saved, hu, hi, hp, own):
    hout, hact, hslope, hlow, hob, hsc, hqkv, hatt, inv, lse, vec, acc0 = saved
    seq, dim = x.shape
    ff = hi.shape[1]
    hid = ff // WIDTHS
    rows = dim // 32
    chunks = scatter_chunks(rows, dim, ff) if own else []
    nc = len(chunks)
    extra = ("oq", "ok", "ov", "oo", "oi", "ou", "os") if own else ()
    names = BWD_IN + BWD_OUT + extra + BWD_SCRATCH

    def kernel(*refs):
        r = named(names, refs)
        if own:
            base = len(names)
            sc = Scatter(chunks, (r.gp, r.gi, r.gu), refs[base : base + 5 * nc], refs[base + 5 * nc : -1])
            packed = refs[-1]
            greet(sc.place)
        nsem = [0]

        def load(pairs):
            cps = []
            for a, b in pairs:
                cps.append(pltpu.make_async_copy(a, b, r.sem.at[nsem[0]]))
                nsem[0] += 1
                cps[-1].start()
            return cps

        def wait(cps):
            for cp in cps:
                cp.wait()

        l_ob = load([(r.hob, r.ob), (r.hact, r.act)])
        l_u = load([(r.hu, r.w), (r.hslope, r.slope)])
        l_low = load([(r.hlow, r.low)])
        outs = (r.gp, r.gi, r.gu)
        flying = [None, None]
        turn = [0]

        def emit(a, value, row, col):
            t = turn[0] % 2
            turn[0] += 1
            if flying[t] is not None:
                flying[t].wait()
            nr, ncol = value.shape
            r.stage[t, :, 0:ncol] = value.astype(BF)
            cp = pltpu.make_async_copy(r.stage.at[t, :, pl.ds(0, ncol)],
                                       outs[a].at[pl.ds(row, nr), pl.ds(col, ncol)], r.gsem.at[t])
            cp.start()
            flying[t] = cp

        def flush():
            for t in range(2):
                if flying[t] is not None:
                    flying[t].wait()
                    flying[t] = None

        U, I, O, Q0, Q1 = ((2 * g, 2 * g + 1) for g in range(5))

        def go(group):
            flush()
            if own:
                for ci in group:
                    sc.start(ci)

        def st(n, group):
            if own:
                for ci in group:
                    if n < 4:
                        (sc.stage1, sc.stage2, sc.stage3)[n - 1](ci)
                    else:
                        a, _, r0, nr, c0, ncol, _ = chunks[ci]
                        (packed, r.oi, r.ou)[a][r0 : r0 + nr, c0 : c0 + ncol] = sc.stage4(ci)

        s = bwd_steps(r, emit)
        s["clear"]()
        wait(l_ob)
        for j in range(WIDTHS):
            s["d_outer"](j)
        go(U)
        l_sc = load([(r.hsc, r.act.at[pl.ds(0, 4 * seq), :])])
        wait(l_u)
        s["inner_back"](0, 1)
        st(1, U)
        s["inner_back"](1, WIDTHS)
        l_i = load([(r.hi.at[:, pl.ds(hid * j, hid)], r.w.at[pl.ds(dim * j, dim), :]) for j in range(WIDTHS)])
        st(2, U)
        wait(l_low)
        s["d_inner"](0)
        s["d_inner"](1)
        st(3, U)
        s["d_inner"](2)
        s["d_inner"](3)
        go(I)
        l_q = load([(r.hqkv, r.low.at[pl.ds(0, 3 * seq), :]), (r.hatt, r.low.at[pl.ds(3 * seq, seq), :])])
        st(4, U)
        wait(l_sc)
        wait(l_i)
        s["first_back"](3)
        st(1, I)
        s["first_back"](2)
        st(2, I)
        s["first_back"](1)
        s["first_back"](0)
        l_p = load([(r.hp.at[:, pl.ds(OUT, dim)], r.w.at[pl.ds(3 * dim, dim), :])])
        l_p2 = load([(r.hp.at[:, pl.ds(3 * HALF * h + HALF * t, HALF)],
                      r.w.at[pl.ds(dim * t, dim), pl.ds(HALF * h, HALF)]) for t in range(3) for h in range(2)])
        st(3, I)
        wait(l_q)
        s["d_output"]()
        wait(l_p)
        s["att_back"]()
        go(O)
        st(4, I)
        s["attention_back"](0, 3)
        st(1, O)
        s["d_qkv"](0)
        go(Q0)
        st(2, O)
        s["attention_back"](3, 6)
        st(1, Q0)
        st(3, O)
        s["d_qkv"](1)
        s["small"]()
        go(Q1)
        st(2, Q0)
        st(4, O)
        wait(l_p2)
        s["input_grad"]()
        st(1, Q1)
        st(3, Q0)
        st(2, Q1)
        st(4, Q0)
        st(3, Q1)
        st(4, Q1)
        if own:
            for t, ref in enumerate((r.oq, r.ok, r.ov)):
                for h in range(2):
                    at = 3 * HALF * h + HALF * t
                    ref[:, HALF * h : HALF * (h + 1)] = packed[:, at : at + HALF]
            r.oo[...] = packed[:, OUT : OUT + dim]
            r.os[...] = packed[:, SMALL:OUT]
            for ci in range(nc):
                sc.finish(ci)

    any_ = pl.BlockSpec(memory_space=pl.ANY)
    vm = pl.BlockSpec(memory_space=pltpu.VMEM)
    S = jax.ShapeDtypeStruct
    V = pltpu.VMEM
    flat = lambda a: a.reshape(-1, a.shape[-1])
    out_shape = [S((seq, dim), F32), S(hp.shape, BF), S(hi.shape, BF), S(hu.shape, BF)]
    scratch = [V((4 * seq, dim), BF), V((10 * seq, hid), BF), V((10 * seq, hid), BF), V((4 * seq, dim), BF),
               V((ff, dim), BF), V((seq, dim), F32), V((24, dim), F32), V((8, dim), F32),
               V((2, dim // 2, dim), BF), pltpu.SemaphoreType.DMA((24,)), pltpu.SemaphoreType.DMA((2,))]
    params = dict(vmem_limit_bytes=67043328)
    if own:
        out_shape += [S((rows, dim), F32)] * 4 + [S((rows, ff), F32), S((4 * rows, dim), F32), S((rows, EXTRA), F32)]
        for count in (16, 16, 8, 4, 3):
            scratch += [V((count, c[3], c[5]), BF) for c in chunks]
        scratch += [pltpu.SemaphoreType.DMA((nc, k)) for k in (16, 16, 16, 8, 8, 4, 4, 3, 3)]
        scratch += [V((rows, hp.shape[1]), F32)]
        params.update(collective_id=2, has_side_effects=True)
    return pl.pallas_call(
        kernel,
        out_shape=out_shape,
        in_specs=[vm] * 7 + [any_] * 10,
        out_specs=[vm, any_, any_, any_] + [vm] * len(extra),
        scratch_shapes=scratch,
        compiler_params=pltpu.CompilerParams(**params),
        name="backward",
    )(x, segc, segr, inv, lse, vec, acc0, flat(hob), flat(hact), flat(hslope), flat(hlow), flat(hsc), hu, hi, hp,
      flat(hqkv), hatt)


def direct(rows):
    return lax.axis_size("dp") == 2 and lax.axis_size("fsdp") == 16 and rows % 8 == 0


def per_device(inputs, segments, out_grads, wq, bq, wk, wv, bv, wo, bo, g1, s1, wi, bi, wu, bu, g2, s2):
    rows, dim = wq.shape
    ff = wi.shape[1]
    per = ff // dim
    small = jnp.stack([bq, bv, bo, g1, s1, bu, g2, s2], axis=1)
    small = jnp.concatenate([small, bi.reshape(rows, per), jnp.zeros((rows, EXTRA - 8 - per), BF)], axis=1)
    cut = [w[:, HALF * h : HALF * (h + 1)] for h in range(2) for w in (wq, wk, wv)]
    packed = jnp.concatenate(cut + [small, wo], axis=1)
    width = packed.shape[1]
    own = direct(rows)
    if own:
        h = 13 * 128
        chunks = [
            (0, rows, 0, rows, 0, h, 0), (0, rows, 0, rows, h, width - h, 1),
            (1, rows, 0, rows, 0, ff // 2, 0), (1, rows, 0, rows, ff // 2, ff // 2, 1),
            (2, 4 * rows, 0, 2 * rows, 0, dim, 0), (2, 4 * rows, 2 * rows, 2 * rows, 0, dim, 1),
        ]
        full, wi_f, wu_f = gather([packed, wi, wu], chunks, 1)
    else:
        full, wi_f, wu_f = [lax.all_gather(a, AXES, axis=0, tiled=True) for a in (packed, wi, wu)]
    x = inputs[0]
    seg = segments[0]
    segc, segr = seg[:, None], seg[None, :]
    saved = forward(x, segc, segr, out_grads[:, 0], full, wi_f, wu_f)
    done = backward(x, segc, segr, saved, wu_f, wi_f, full, own)
    x_grad = done[0]
    if own:
        gq, gk, gv, go, gi, gu, rs = done[4:]
    else:
        red, gi, gu = [lax.psum_scatter(a, AXES, scatter_dimension=0, tiled=True).astype(F32) for a in done[1:4]]
        gq, gk, gv = [
            jnp.concatenate([red[:, 3 * HALF * h + HALF * t :][:, :HALF] for h in range(2)], axis=1) for t in range(3)
        ]
        rs, go = red[:, SMALL:OUT], red[:, OUT:]
    vecs = [rs[:, i] for i in range(8)]
    gb = rs[:, 8 : 8 + per].reshape(-1)
    return (saved[0][:, None], x_grad[None], gq, vecs[0], gk, gv, vecs[1], go, vecs[2], vecs[3], vecs[4], gi, gb, gu,
            vecs[5], vecs[6], vecs[7])


def solution(mesh):
    mat = P(AXES, None)
    vec = P(AXES)
    params = (mat, vec, mat, mat, vec, mat, vec, vec, vec, mat, vec, mat, vec, vec, vec)
    return jax.shard_map(
        per_device,
        mesh=mesh,
        in_specs=(P(AXES, None, None), P(AXES, None), P(None, AXES, None, None)) + params,
        out_specs=(P(None, AXES, None, None), P(AXES, None, None)) + params,
        check_vma=False,
    )
```

profile of v0, /device:TPU:0, one launch (start us, length us, event | category | flops | bytes accessed | tf_op | source)
XLA Modules:
  0.0 315.4 jit_solution(13848529398325137071)
XLA Ops:
  0.7 0.7 copy.44
  1.4 0.7 copy.45
  2.1 0.7 copy.46
  2.9 0.7 copy.47
  3.6 0.7 copy.48
  4.4 0.7 reshape.58
  5.1 0.8 copy.49
  5.9 0.7 copy.50
  6.6 0.7 copy.51
  7.4 0.7 fusion.2
  8.1 0.8 fusion
  8.9 1.5 concatenate.3.refs_0_
  10.5 1.5 copy.52.refs_1_
  12.0 74.0 %gather.1 = (bf16[768,3200]{1,0:T(8,128)(2,1)}, bf16[768,3072]{1,0:T(8,128)(2,1)}, bf16[3072,768]{1,0:T(8,128)(2,1)}) custom-call(bf16[24,3200]{1,0:T(8,128)(2,1)} %concatenate.3.refs_0_, bf16[24,3072]{1,0:T(8,128)(2,1)} %refs_1_.1, bf16[96,768]{1,0:T(8,128)(2,1)} %refs_2_.3), custom_call_target="tpu_custom_call" | custom-call | tf_op jit(solution)/shard_map/gather/pallas_call | solution.py:185
  86.0 62.9 %forward.1 = (bf16[4,512,768]{2,1,0:T(8,128)(2,1)}, bf16[10,512,768]{2,1,0:T(8,128)(2,1)}, bf16[10,512,768]{2,1,0:T(8,128)(2,1)}, bf16[4,512,768]{2,1,0:T(8,128)...) custom-call(bf16[512,768]{1,0:T(8,128)(2,1)} %bitcast.27, ...), custom_call_target="tpu_custom_call" | custom-call | tf_op jit(solution)/shard_map/forward/pallas_call | solution.py:407
  148.9 150.9 %backward.1 = (f32[512,768]{1,0:T(8,128)}, bf16[768,3200]{1,0:T(8,128)(2,1)}, bf16[768,3072]{1,0:T(8,128)(2,1)}, bf16[3072,768]{1,0:T(8,128)(2,1)}, f32[24,768]{...) custom-call(bf16[512,768]{1,0:T(8,128)(2,1)} %bitcast.28, ...), custom_call_target="tpu_custom_call" | custom-call | tf_op jit(solution)/shard_map/backward/pallas_call | solution.py:856
  299.8 1.8 slice_reduce_fusion
  301.6 0.8 slice.56
  302.4 0.6 reshape.65
  303.0 2.7 copy.62
  305.7 1.5 copy.63
  307.2 1.5 copy.64
  308.7 1.5 copy.65
  310.2 1.5 copy.66
  311.8 1.7 copy.67
  313.5 1.7 copy.68
  (1 shorter events, 0.0 us)
where the time goes:
time: 321 us; the launch traced here: 315 us
  Pallas kernels  288 us (90%)
  local copies, waits for them, and re-layouts  26.7 us (8%)
    pallas_call x1, Pallas kernels, backward(): pl.pallas_call(kernel, out_shape=out_shape, in_specs=[vm] * 7 + [any_] *...  151 us
    pallas_call x1, Pallas kernels, gather(): pl.pallas_call(kernel, out_shape=[jax.ShapeDtypeStruct((32 * a.shape[0],...  74 us
    pallas_call x1, Pallas kernels, forward(): pl.pallas_call(kernel, out_shape=out_shape, in_specs=[vm, vm, vm, vm, any...  62.9 us
    unnamed x7, local copies, waits for them, and re-layouts  12.1 us

commit v1 on v0

--- a/solution.py
+++ b/solution.py
@@ -773,58 +773,57 @@
         go(U)
         l_sc = load([(r.hsc, r.act.at[pl.ds(0, 4 * seq), :])])
         wait(l_u)
-        s["inner_back"](0, 1)
+        s["inner_back"](0, WIDTHS)
+        l_i = load([(r.hi.at[:, pl.ds(hid * j, hid)], r.w.at[pl.ds(dim * j, dim), :]) for j in range(WIDTHS)])
         st(1, U)
-        s["inner_back"](1, WIDTHS)
-        l_i = load([(r.hi.at[:, pl.ds(hid * j, hid)], r.w.at[pl.ds(dim * j, dim), :]) for j in range(WIDTHS)])
-        st(2, U)
         wait(l_low)
-        s["d_inner"](0)
-        s["d_inner"](1)
-        st(3, U)
-        s["d_inner"](2)
-        s["d_inner"](3)
+        for j in range(WIDTHS):
+            s["d_inner"](j)
         go(I)
         l_q = load([(r.hqkv, r.low.at[pl.ds(0, 3 * seq), :]), (r.hatt, r.low.at[pl.ds(3 * seq, seq), :])])
-        st(4, U)
         wait(l_sc)
         wait(l_i)
         s["first_back"](3)
+        st(2, U)
+        s["first_back"](2)
         st(1, I)
-        s["first_back"](2)
-        st(2, I)
         s["first_back"](1)
+        st(3, U)
         s["first_back"](0)
         l_p = load([(r.hp.at[:, pl.ds(OUT, dim)], r.w.at[pl.ds(3 * dim, dim), :])])
         l_p2 = load([(r.hp.at[:, pl.ds(3 * HALF * h + HALF * t, HALF)],
                       r.w.at[pl.ds(dim * t, dim), pl.ds(HALF * h, HALF)]) for t in range(3) for h in range(2)])
-        st(3, I)
         wait(l_q)
         s["d_output"]()
+        go(O)
         wait(l_p)
         s["att_back"]()
-        go(O)
-        st(4, I)
-        s["attention_back"](0, 3)
+        s["attention_back"](0, 2)
+        st(2, I)
         st(1, O)
+        s["attention_back"](2, 3)
         s["d_qkv"](0)
         go(Q0)
+        st(4, U)
+        s["attention_back"](3, 5)
+        st(3, I)
         st(2, O)
-        s["attention_back"](3, 6)
         st(1, Q0)
-        st(3, O)
+        s["attention_back"](5, 6)
         s["d_qkv"](1)
         s["small"]()
         go(Q1)
-        st(2, Q0)
-        st(4, O)
+        st(3, O)
         wait(l_p2)
         s["input_grad"]()
         st(1, Q1)
+        st(4, I)
+        st(2, Q0)
+        st(4, O)
+        st(2, Q1)
         st(3, Q0)
-        st(2, Q1)
+        st(3, Q1)
         st(4, Q0)
-        st(3, Q1)
         st(4, Q1)
         if own:
             for t, ref in enumerate((r.oq, r.ok, r.ov)):
@@ -865,6 +864,22 @@
       flat(hqkv), hatt)
 
 
+def settle(arrays):
+    n = len(arrays)
+
+    def kernel(*refs):
+        for a, b in zip(refs[:n], refs[n:]):
+            b[...] = a[...]
+
+    return pl.pallas_call(
+        kernel,
+        out_shape=[jax.ShapeDtypeStruct(a.shape, a.dtype) for a in arrays],
+        in_specs=[pl.BlockSpec(memory_space=pltpu.VMEM)] * n,
+        out_specs=[pl.BlockSpec(memory_space=pltpu.VMEM)] * n,
+        name="settle",
+    )(*arrays)
+
+
 def direct(rows):
     return lax.axis_size("dp") == 2 and lax.axis_size("fsdp") == 16 and rows % 8 == 0
 
@@ -896,7 +911,7 @@
     done = backward(x, segc, segr, saved, wu_f, wi_f, full, own)
     x_grad = done[0]
     if own:
-        gq, gk, gv, go, gi, gu, rs = done[4:]
+        x_grad, gq, gk, gv, go, gi, gu, rs = settle([x_grad] + list(done[4:]))
     else:
         red, gi, gu = [lax.psum_scatter(a, AXES, scatter_dimension=0, tiled=True).astype(F32) for a in done[1:4]]
         gq, gk, gv = [

time: 321 us -> 287 us (0.89)
  Pallas kernels: 288 us -> 266 us
  local copies, waits for them, and re-layouts: 26.7 us -> 14.6 us
    pallas_call x1, Pallas kernels: 151 us -> 126 us  [backward(): pl.pallas_call(kernel, out_shape=out_shape, in_specs=[vm] * 7 + [any_] *...]
    unnamed x7 -> x0, local copies, waits for them, and re-layouts: 12.1 us -> none
where the time goes in v1:
time: 287 us; the launch traced here: 282 us
  Pallas kernels  266 us (93%)
  local copies, waits for them, and re-layouts  14.6 us (5%)
    pallas_call x1, Pallas kernels, backward(): pl.pallas_call(kernel, out_shape=out_shape, in_specs=[vm] * 7 + [any_] *...  126 us
    pallas_call x1, Pallas kernels, gather(): pl.pallas_call(kernel, out_shape=[jax.ShapeDtypeStruct((32 * a.shape[0],...  74 us
    pallas_call x1, Pallas kernels, forward(): pl.pallas_call(kernel, out_shape=out_shape, in_specs=[vm, vm, vm, vm, any...  62.9 us
    another operation x8, local copies, waits for them, and re-layouts, per_device(): small = jnp.stack([bq, bv, bo, g1, s1, bu, g2, s2], axis=1)  5.98 us

profile of v1, /device:TPU:0, one launch (start us, length us, event | category | flops | bytes accessed | tf_op | source)
XLA Modules:
  0.0 281.9 jit_solution(8718472311209377917)
XLA Ops:
  0.7 0.7 copy.44
  1.4 0.7 copy.45
  2.1 0.7 copy.46
  2.9 0.7 copy.47
  3.6 0.7 copy.48
  4.4 0.7 reshape.58
  5.1 0.8 copy.49
  5.9 0.7 copy.50
  6.6 0.7 copy.51
  7.4 0.7 fusion.2
  8.1 0.8 fusion
  8.9 1.5 concatenate.3.refs_0_
  10.5 1.5 copy.52.refs_1_
  12.0 74.0 %gather.1 = (bf16[768,3200]{1,0:T(8,128)(2,1)}, bf16[768,3072]{1,0:T(8,128)(2,1)}, bf16[3072,768]{1,0:T(8,128)(2,1)}) custom-call(bf16[24,3200]{1,0:T(8,128)(2,1)} %concatenate.3.refs_0_, bf16[24,3072]{1,0:T(8,128)(2,1)} %refs_1_.1, bf16[96,768]{1,0:T(8,128)(2,1)} %refs_2_.3), custom_call_target="tpu_custom_call" | custom-call | tf_op jit(solution)/shard_map/gather/pallas_call | solution.py:185
  86.0 62.9 %forward.1 = (bf16[4,512,768]{2,1,0:T(8,128)(2,1)}, bf16[10,512,768]{2,1,0:T(8,128)(2,1)}, bf16[10,512,768]{2,1,0:T(8,128)(2,1)}, bf16[4,512,768]{2,1,0:T(8,128)...) custom-call(bf16[512,768]{1,0:T(8,128)(2,1)} %bitcast.27, ...), custom_call_target="tpu_custom_call" | custom-call | tf_op jit(solution)/shard_map/forward/pallas_call | solution.py:407
  148.9 126.2 %backward.1 = (f32[512,768]{1,0:T(8,128)}, bf16[768,3200]{1,0:T(8,128)(2,1)}, bf16[768,3072]{1,0:T(8,128)(2,1)}, bf16[3072,768]{1,0:T(8,128)(2,1)}, f32[24,768]{...) custom-call(bf16[512,768]{1,0:T(8,128)(2,1)} %bitcast.28, ...), custom_call_target="tpu_custom_call" | custom-call | tf_op jit(solution)/shard_map/backward/pallas_call | solution.py:855
  275.1 3.1 %settle.1 = (f32[512,768]{1,0:T(8,128)}, f32[24,768]{1,0:T(8,128)}, f32[24,768]{1,0:T(8,128)}, f32[24,768]{1,0:T(8,128)}, f32[24,768]{1,0:T(8,128)}, /*index=5*/...) custom-call(f32[512,768]{1,0:T(8,128)} %get-tuple-element.63.refs_0_, f32[24,768]{1,0:T(8,128)} %get-tuple-element.64.refs_1_, ...), custom_call_target="tpu_custom_call" | custom-call | tf_op jit(solution)/shard_map/settle/pallas_call | solution.py:874
  278.2 1.8 slice_reduce_fusion
  280.0 0.8 slice.56
  280.8 0.6 reshape.65
  (1 shorter events, 0.0 us)
